TPU v7x, 32 devices: a whole 2x2x4 slice. The times are simulated.
32 devices in a mesh: prow: 4 (over z), pcol: 8 (over y, x, core).
Axes of the slice: x: 2, y: 2, z: 4, core: 2. Of those that a mesh axis runs over, the one named last changes fastest.
Arguments:
- tiles: bfloat16 [4, 8, 32, 256, 256], P('prow', 'pcol')
- tile_brow: int32 [4, 8, 32], P('prow', 'pcol'), may hold values from 0 to 31, as said below
- tile_bcol: int32 [4, 8, 32], P('prow', 'pcol'), may hold values from 0 to 15, as said below
- tile_count: int32 [4, 8], P('prow', 'pcol'), may hold values from 8 to 32, as said below
Outputs:
- row_scale: float32 [32, 4, 256], P(None, 'prow')
- col_scale: float32 [16, 8, 256], P(None, 'pcol')
Inputs may be any that keep to these rules, and one draw needn't show every extreme that they name: `tile_brow`: on one device, no two slots name the same pair of local block row and column; the diagonal tile of every block row is present and live, in the first slots of the device that holds it. `tile_bcol`: see tile_brow. `tile_count`: a device that holds diagonal tiles has all 32 slots live, every other device at most 16.
All inputs are finite; a program needn't handle non-finite values.
Results may differ from a plain program's by a relative error of at most 0.0003.
Values sent between devices are 32-bit elements; how exact they have to be, the bound alone decides.
A program may use at most 64 MiB of HBM per device.

v0:
```python
import jax
import jax.numpy as jnp
from jax import lax
from jax.sharding import PartitionSpec as P

BR_DEV = 32
SWEEPS = 3


def rescale(scale, largest):
    return scale / jnp.sqrt(largest)


def on_device(tiles, tile_brow, tile_bcol, tile_count):
    slots = tiles.shape[2]
    width = tiles.shape[3]
    col_blocks = BR_DEV * lax.axis_size("prow") // lax.axis_size("pcol")
    brow = tile_brow.reshape(slots)
    bcol = tile_bcol.reshape(slots)
    alive = (jnp.arange(slots, dtype=jnp.int32) < tile_count.reshape(1)).astype(jnp.float32)
    block = tiles.reshape(slots, width, width)
    row_vec = jnp.ones((BR_DEV, width), jnp.float32)
    col_vec = jnp.ones((col_blocks, width), jnp.float32)
    brow_float = brow.astype(jnp.float32).reshape(1, 1, slots)
    bcol_float = bcol.astype(jnp.float32).reshape(1, 1, slots)

    def fold_rows(carry, pieces):
        places = pieces[0].reshape(-1).astype(jnp.int32)
        return carry.at[places].max(pieces[1].reshape(-1, width))

    for sweep in range(SWEEPS):
        scaled = (
            jnp.abs(block.astype(jnp.float32))
            * row_vec[brow][:, :, None]
            * col_vec[bcol][:, None, :]
        )
        row_part = jnp.max(scaled, axis=2) * alive[:, None]
        col_part = jnp.max(scaled, axis=1) * alive[:, None]
        row_max = fold_rows(
            jnp.zeros((BR_DEV, width), jnp.float32),
            (
                lax.all_gather(brow_float, "pcol", axis=1, tiled=True),
                lax.all_gather(row_part.reshape(1, 1, slots, width), "pcol", axis=1, tiled=True),
            ),
        )
        col_max = fold_rows(
            jnp.zeros((col_blocks, width), jnp.float32),
            (
                lax.all_gather(bcol_float, "prow", axis=0, tiled=True),
                lax.all_gather(col_part.reshape(1, 1, slots, width), "prow", axis=0, tiled=True),
            ),
        )
        row_vec = rescale(row_vec, row_max)
        col_vec = rescale(col_vec, col_max)
    return (row_vec.reshape(BR_DEV, 1, width), col_vec.reshape(col_blocks, 1, width))


def solution(mesh):
    return jax.shard_map(
        on_device,
        mesh=mesh,
        in_specs=(
            P("prow", "pcol", None, None, None),
            P("prow", "pcol", None),
            P("prow", "pcol", None),
            P("prow", "pcol"),
        ),
        out_specs=(P(None, "prow", None), P(None, "pcol", None)),
        check_vma=False,
    )
```

profile of v0, /device:TPU:0, one launch (start us, length us, event | category | flops | bytes accessed | tf_op | source)
XLA Modules:
  0.0 123.1 jit_solution(12357050907770973232)
XLA Ops:
  1.3 0.7 fusion.24
  1.9 0.7 bitcast_convert_fusion
  2.6 0.7 convert_element_type.56
  3.3 0.7 fusion.25
  3.9 12.6 %all_gather.30 = f32[4,1,32]{2,1,0:T(1,128)S(1)} all-gather(f32[1,1,32]{2,1,0:T(1,128)S(1)} %convert_element_type.56), channel_id=1, replica_groups=mesh['prow'=4,'pcol'=8] {'prow'}, dimensions={0}, use_global_device_ids=true | all-gather | bytes 640 | tf_op jit(solution)/shard_map/all_gather | solution.py:49
  16.6 0.1 convert_element_type.58
  16.7 8.8 %all_gather.28 = f32[1,8,32]{2,0,1:T(1,128)S(1)} all-gather(f32[1,1,32]{2,0,1:T(1,128)S(1)} %bitcast_convert_fusion), channel_id=1, replica_groups=mesh['prow'=4,'pcol'=8] {'pcol'}, dimensions={1}, use_global_device_ids=true | all-gather | bytes 1152 | tf_op jit(solution)/shard_map/all_gather | solution.py:42
  25.5 0.1 convert_element_type.53
  25.6 0.6 gather_fusion.1
  26.2 0.6 gather_fusion
  26.8 5.1 %fusion.8 = (f32[32,256]{1,0:T(8,128)S(1)}, f32[32,256]{1,0:T(8,128)S(1)}) fusion(bf16[1,1,32,256,256]{4,3,2,1,0:T(8,128)(2,1)} %param.4, f32[32,256]{1,0:T(8,128)S(1)} %gather_fusion.1, f32[32,256]{1,0:T(8,128)S(1)} %gather_fusion), kind=kLoop, calls=%fused_computation.24 | loop fusion | flops 12566528 | bytes 4325376 | tf_op jit(solution)/shard_map/reduce_max | solution.py:37
  31.9 0.1 bitcast_multiply_fusion.8
  32.0 13.4 %all_gather.31 = f32[4,1,32,256]{3,2,1,0:T(8,128)S(1)} all-gather(f32[1,1,32,256]{3,2,1,0:T(8,128)S(1)} %get-tuple-element.17), channel_id=1, replica_groups=mesh['prow'=4,'pcol'=8] {'prow'}, dimensions={0}, use_global_device_ids=true | all-gather | bytes 163840 | tf_op jit(solution)/shard_map/all_gather | solution.py:50
  45.4 1.3 %scatter_custom_fusion.1 = f32[16,256]{1,0:T(8,128)S(1)} fusion(s32[128]{0:T(128)S(1)} %fusion.26, f32[128,256]{1,0:T(8,128)S(1)} %bitcast.75, f32[]{:T(128)} %constant.6.clone.1), kind=kCustom, calls=%fused_computation.48 | custom fusion | flops 32768 | bytes 16388 | tf_op jit(solution)/shard_map/scatter-max | solution.py:29
  46.7 0.6 gather_fusion.3
  47.3 9.3 %all_gather.29 = f32[1,8,32,256]{3,2,0,1:T(8,128)S(1)} all-gather(f32[1,1,32,256]{3,2,0,1:T(8,128)S(1)} %get-tuple-element.16), channel_id=1, replica_groups=mesh['prow'=4,'pcol'=8] {'pcol'}, dimensions={1}, use_global_device_ids=true | all-gather | bytes 294912 | tf_op jit(solution)/shard_map/all_gather | solution.py:43
  56.5 2.0 %scatter_custom_fusion = f32[32,256]{1,0:T(8,128)S(1)} fusion(s32[256]{0:T(256)S(1)} %bitcast.77, f32[256,256]{1,0:T(8,128)S(1)} %bitcast.72, f32[]{:T(128)} %constant.6.clone.1), kind=kCustom, calls=%fused_computation.42 | custom fusion | flops 65536 | bytes 32772 | tf_op jit(solution)/shard_map/scatter-max | solution.py:29
  58.5 0.6 gather_fusion.2
  59.1 5.1 %fusion.5 = (f32[32,256]{1,0:T(8,128)S(1)}, f32[32,256]{1,0:T(8,128)S(1)}) fusion(bf16[1,1,32,256,256]{4,3,2,1,0:T(8,128)(2,1)} %param.4, f32[32,256]{1,0:T(8,128)S(1)} %gather_fusion.3, f32[32,256]{1,0:T(8,128)S(1)} %gather_fusion.2), kind=kLoop, calls=%fused_computation.21 | loop fusion | flops 12566528 | bytes 4325376 | tf_op jit(solution)/shard_map/reduce_max | solution.py:38
  64.2 0.1 fusion.10
  64.3 13.4 %all_gather.33 = f32[4,1,32,256]{3,2,1,0:T(8,128)S(1)} all-gather(f32[1,1,32,256]{3,2,1,0:T(8,128)S(1)} %get-tuple-element.14), channel_id=1, replica_groups=mesh['prow'=4,'pcol'=8] {'prow'}, dimensions={0}, use_global_device_ids=true | all-gather | bytes 163840 | tf_op jit(solution)/shard_map/all_gather | solution.py:50
  77.7 1.3 %scatter_custom_fusion.3 = f32[16,256]{1,0:T(8,128)S(1)} fusion(s32[128]{0:T(128)S(1)} %fusion.26, f32[128,256]{1,0:T(8,128)S(1)} %bitcast.76, f32[]{:T(128)} %constant.6.clone.1), kind=kCustom, calls=%fused_computation.46 | custom fusion | flops 32768 | bytes 16388 | tf_op jit(solution)/shard_map/scatter-max | solution.py:29
  79.0 0.6 gather_fusion.5
  79.6 8.3 %all_gather.32 = f32[1,8,32,256]{3,2,0,1:T(8,128)S(1)} all-gather(f32[1,1,32,256]{3,2,0,1:T(8,128)S(1)} %get-tuple-element.15), channel_id=1, replica_groups=mesh['prow'=4,'pcol'=8] {'pcol'}, dimensions={1}, use_global_device_ids=true | all-gather | bytes 294912 | tf_op jit(solution)/shard_map/all_gather | solution.py:43
  87.9 2.0 %scatter_custom_fusion.2 = f32[32,256]{1,0:T(8,128)S(1)} fusion(s32[256]{0:T(256)S(1)} %bitcast.78, f32[256,256]{1,0:T(8,128)S(1)} %bitcast.73, f32[]{:T(128)} %constant.6.clone.1), kind=kCustom, calls=%fused_computation.40 | custom fusion | flops 65536 | bytes 32772 | tf_op jit(solution)/shard_map/scatter-max | solution.py:29
  89.9 0.6 gather_fusion.4
  90.5 5.1 %fusion.3 = (f32[32,256]{1,0:T(8,128)S(1)}, f32[32,256]{1,0:T(8,128)S(1)}) fusion(bf16[1,1,32,256,256]{4,3,2,1,0:T(8,128)(2,1)} %param.4, f32[32,256]{1,0:T(8,128)S(1)} %gather_fusion.5, f32[32,256]{1,0:T(8,128)S(1)} %gather_fusion.4), kind=kLoop, calls=%fused_computation.19 | loop fusion | flops 12566528 | bytes 4325376 | tf_op jit(solution)/shard_map/reduce_max | solution.py:38
  95.6 0.1 fusion.9
  95.7 13.6 %all_gather.35 = f32[4,1,32,256]{3,2,1,0:T(8,128)S(1)} all-gather(f32[1,1,32,256]{3,2,1,0:T(8,128)S(1)} %get-tuple-element.12), channel_id=1, replica_groups=mesh['prow'=4,'pcol'=8] {'prow'}, dimensions={0}, use_global_device_ids=true | all-gather | bytes 163840 | tf_op jit(solution)/shard_map/all_gather | solution.py:50
  109.3 1.3 %scatter_custom_fusion.5 = f32[16,256]{1,0:T(8,128)S(1)} fusion(s32[128]{0:T(128)S(1)} %fusion.26, f32[128,256]{1,0:T(8,128)S(1)} %bitcast.74, f32[]{:T(128)} %constant.6.clone.1), kind=kCustom, calls=%fused_computation.44 | custom fusion | flops 32768 | bytes 16388 | tf_op jit(solution)/shard_map/scatter-max | solution.py:29
  110.6 0.6 copy.13
  111.2 9.3 %all_gather.34 = f32[1,8,32,256]{3,2,0,1:T(8,128)S(1)} all-gather(f32[1,1,32,256]{3,2,0,1:T(8,128)S(1)} %get-tuple-element.13), channel_id=1, replica_groups=mesh['prow'=4,'pcol'=8] {'pcol'}, dimensions={1}, use_global_device_ids=true | all-gather | bytes 294912 | tf_op jit(solution)/shard_map/all_gather | solution.py:43
  120.4 2.0 %scatter_custom_fusion.4 = f32[32,256]{1,0:T(8,128)S(1)} fusion(s32[256]{0:T(256)S(1)} %bitcast.79, f32[256,256]{1,0:T(8,128)S(1)} %bitcast.71, f32[]{:T(128)} %constant.6.clone.1), kind=kCustom, calls=%fused_computation.38 | custom fusion | flops 65536 | bytes 32772 | tf_op jit(solution)/shard_map/scatter-max | solution.py:29
  122.4 0.6 copy.12
  (15 shorter events, 0.1 us)
where the time goes:
time: 123 us
  blocking collectives  88.6 us (72%)
  other arithmetic  27.9 us (23%)
  local copies, waits for them, and re-layouts  5.07 us (4%)
  between operations  1.45 us (1%)
    all_gather x3, blocking collectives, on_device(): lax.all_gather(col_part.reshape(1, 1, slots, width), 'prow', axis=0, tile...  40.3 us
    all_gather x3, blocking collectives, on_device(): lax.all_gather(row_part.reshape(1, 1, slots, width), 'pcol', axis=1, tile...  26.9 us
    all_gather x1, blocking collectives, on_device(): lax.all_gather(bcol_float, 'prow', axis=0, tiled=True)  12.6 us
    reduce_max x2, other arithmetic, on_device(): col_part = jnp.max(scaled, axis=1) * alive[:, None]  10.2 us
    another operation x6, other arithmetic, fold_rows(): return carry.at[places].max(pieces[1].reshape(-1, width))  9.63 us
    all_gather x1, blocking collectives, on_device(): lax.all_gather(brow_float, 'pcol', axis=1, tiled=True)  8.8 us
    reduce_max x1, other arithmetic, on_device(): row_part = jnp.max(scaled, axis=2) * alive[:, None]  5.1 us

commit v1 on v0

v1 whole, which is shorter than its diff:
```python
import functools

import jax
import jax.numpy as jnp
from jax import lax
from jax.experimental import pallas as pl
from jax.experimental.pallas import tpu as pltpu
from jax.sharding import PartitionSpec as P

BR_DEV = 32
SWEEPS = 3
LANES = 128
LOADS = 8


def rescale(scale, largest):
    return scale / jnp.sqrt(largest)


def kernel(
    n_prow, n_pcol, col_blocks, slots, width,
    brow_ref, bcol_ref, count_ref, tiles_ref,
    row_out, col_out,
    block, row_split, col_vec, row_send, col_send, row_recv, col_recv,
    load_sem, row_send_sem, row_recv_sem, col_send_sem, col_recv_sem,
):
    per = slots // LOADS
    loads = [
        pltpu.make_async_copy(
            tiles_ref.at[pl.ds(i * per, per)], block.at[pl.ds(i * per, per)], load_sem.at[i]
        )
        for i in range(LOADS)
    ]
    for load in loads:
        load.start()

    pr = lax.axis_index("prow")
    pc = lax.axis_index("pcol")
    barrier = pltpu.get_barrier_semaphore()
    for d in range(1, n_pcol):
        pl.semaphore_signal(barrier, inc=1, device_id={"pcol": lax.rem(pc + d, n_pcol)})
    for d in range(1, n_prow):
        pl.semaphore_signal(barrier, inc=1, device_id={"prow": lax.rem(pr + d, n_prow)})

    count = count_ref[0]
    row_ids = lax.broadcasted_iota(jnp.int32, (BR_DEV, width), 0)
    col_ids = lax.broadcasted_iota(jnp.int32, (col_blocks, width), 0)
    lane_ids = lax.broadcasted_iota(jnp.int32, (1, LANES), 1)
    ones = jnp.ones((LANES, LANES), jnp.bfloat16)
    step = 16
    halves = width // LANES

    def one_tile(s, carry, first):
        row_acc, col_acc = carry
        brow = brow_ref[s]
        bcol = bcol_ref[s]
        if not first:
            pick = jnp.where(
                (lane_ids % BR_DEV == brow) & (lane_ids < 3 * BR_DEV), 1.0, 0.0
            ).astype(jnp.bfloat16)
            spread = jnp.dot(
                row_split[...] * pick, ones, preferred_element_type=jnp.float32
            )
            cols = col_vec[pl.ds(bcol, 1), :]
        col_part = [jnp.zeros((step, LANES), jnp.float32) for _ in range(halves)]
        pieces = []
        for g in range(width // step):
            best = None
            for h in range(halves):
                x = jnp.abs(
                    block[s, g * step:(g + 1) * step, h * LANES:(h + 1) * LANES].astype(jnp.float32)
                )
                if not first:
                    x = x * spread[g * step:(g + 1) * step]
                    x = x * cols[:, h * LANES:(h + 1) * LANES]
                col_part[h] = jnp.maximum(col_part[h], x)
                best = x if best is None else jnp.maximum(best, x)
            pieces.append(best)
        parts = []
        for h in range(halves):
            part = jnp.concatenate(pieces[h * LANES // step:(h + 1) * LANES // step], axis=0)
            parts.append(jnp.max(part.T, axis=0, keepdims=True))
        row_part = jnp.concatenate(parts, axis=1)
        col_top = jnp.concatenate([jnp.max(c, axis=0, keepdims=True) for c in col_part], axis=1)
        alive = s < count
        row_at = jnp.where(alive, brow, -1)
        col_at = jnp.where(alive, bcol, -1)
        row_acc = jnp.maximum(row_acc, jnp.where(row_ids == row_at, row_part, 0.0))
        col_acc = jnp.maximum(col_acc, jnp.where(col_ids == col_at, col_top, 0.0))
        return row_acc, col_acc

    row_vec = jnp.ones((BR_DEV, width), jnp.float32)
    col_now = jnp.ones((col_blocks, width), jnp.float32)
    for sweep in range(SWEEPS):
        carry = (
            jnp.zeros((BR_DEV, width), jnp.float32),
            jnp.zeros((col_blocks, width), jnp.float32),
        )
        body = functools.partial(one_tile, first=sweep == 0)
        if sweep == 0:
            for i in range(LOADS):
                loads[i].wait()
                carry = lax.fori_loop(i * per, (i + 1) * per, body, carry)
        else:
            carry = lax.fori_loop(0, slots, body, carry)
        row_max, col_max = carry
        col_send[sweep] = col_max
        row_send[sweep] = row_max
        if sweep == 0:
            pl.semaphore_wait(barrier, n_pcol - 1 + n_prow - 1)
        copies = []
        for d in range(1, n_prow):
            copies.append(pltpu.make_async_remote_copy(
                src_ref=col_send.at[sweep], dst_ref=col_recv.at[sweep, d - 1],
                send_sem=col_send_sem.at[sweep, d - 1], recv_sem=col_recv_sem.at[sweep, d - 1],
                device_id={"prow": lax.rem(pr + d, n_prow)},
            ))
        for d in range(1, n_pcol):
            copies.append(pltpu.make_async_remote_copy(
                src_ref=row_send.at[sweep], dst_ref=row_recv.at[sweep, d - 1],
                send_sem=row_send_sem.at[sweep, d - 1], recv_sem=row_recv_sem.at[sweep, d - 1],
                device_id={"pcol": lax.rem(pc + d, n_pcol)},
            ))
        for copy in copies:
            copy.start()
        for copy in copies:
            copy.wait()
        for d in range(1, n_prow):
            col_max = jnp.maximum(col_max, col_recv[sweep, d - 1])
        for d in range(1, n_pcol):
            row_max = jnp.maximum(row_max, row_recv[sweep, d - 1])
        row_vec = rescale(row_vec, row_max)
        col_now = rescale(col_now, col_max)
        if sweep + 1 < SWEEPS:
            col_vec[...] = col_now
            top = row_vec.astype(jnp.bfloat16).astype(jnp.float32)
            left = row_vec - top
            mid = left.astype(jnp.bfloat16).astype(jnp.float32)
            low = left - mid
            rest = jnp.zeros((LANES - 3 * BR_DEV, width), jnp.float32)
            stack = jnp.concatenate([top, mid, low, rest], axis=0)
            for h in range(halves):
                row_split[h * LANES:(h + 1) * LANES, :] = (
                    stack[:, h * LANES:(h + 1) * LANES].T.astype(jnp.bfloat16)
                )
    row_out[...] = row_vec
    col_out[...] = col_now


def solution(mesh):
    n_prow, n_pcol = mesh.shape["prow"], mesh.shape["pcol"]

    def on_device(tiles, tile_brow, tile_bcol, tile_count):
        slots, width = tiles.shape[2], tiles.shape[3]
        col_blocks = BR_DEV * n_prow // n_pcol
        smem = pl.BlockSpec(memory_space=pltpu.SMEM)
        vmem = pl.BlockSpec(memory_space=pltpu.VMEM)
        row_vec, col_vec = pl.pallas_call(
            functools.partial(kernel, n_prow, n_pcol, col_blocks, slots, width),
            out_shape=(
                jax.ShapeDtypeStruct((BR_DEV, width), jnp.float32),
                jax.ShapeDtypeStruct((col_blocks, width), jnp.float32),
            ),
            in_specs=[smem, smem, smem, pl.BlockSpec(memory_space=pl.ANY)],
            out_specs=(vmem, vmem),
            scratch_shapes=[
                pltpu.VMEM((slots, width, width), jnp.bfloat16),
                pltpu.VMEM((width, LANES), jnp.bfloat16),
                pltpu.VMEM((col_blocks, width), jnp.float32),
                pltpu.VMEM((SWEEPS, BR_DEV, width), jnp.float32),
                pltpu.VMEM((SWEEPS, col_blocks, width), jnp.float32),
                pltpu.VMEM((SWEEPS, n_pcol - 1, BR_DEV, width), jnp.float32),
                pltpu.VMEM((SWEEPS, n_prow - 1, col_blocks, width), jnp.float32),
                pltpu.SemaphoreType.DMA((LOADS,)),
                pltpu.SemaphoreType.DMA((SWEEPS, n_pcol - 1)),
                pltpu.SemaphoreType.DMA((SWEEPS, n_pcol - 1)),
                pltpu.SemaphoreType.DMA((SWEEPS, n_prow - 1)),
                pltpu.SemaphoreType.DMA((SWEEPS, n_prow - 1)),
            ],
            compiler_params=pltpu.CompilerParams(collective_id=0, has_side_effects=True),
        )(
            tile_brow.reshape(slots), tile_bcol.reshape(slots), tile_count.reshape(1),
            tiles.reshape(slots, width, width),
        )
        return (row_vec.reshape(BR_DEV, 1, width), col_vec.reshape(col_blocks, 1, width))

    return jax.shard_map(
        on_device,
        mesh=mesh,
        in_specs=(
            P("prow", "pcol", None, None, None),
            P("prow", "pcol", None),
            P("prow", "pcol", None),
            P("prow", "pcol"),
        ),
        out_specs=(P(None, "prow", None), P(None, "pcol", None)),
        check_vma=False,
    )
```

time: 123 us -> 44.5 us (0.36)
  blocking collectives: 88.6 us -> 0 us
  Pallas kernels: 0 us -> 40.2 us
  other arithmetic: 27.9 us -> 0 us
  local copies, waits for them, and re-layouts: 5.07 us -> 2.75 us
    all_gather x8 -> x0, blocking collectives: 88.6 us -> none  [the longest x3 40.3 us: on_device(): lax.all_gather(col_part.reshape(1, 1, slots, width), 'prow', axis=0, tile...]
    pallas_call x0 -> x1, Pallas kernels: none -> 40.2 us  [on_device(): pl.pallas_call(functools.partial(kernel, n_prow, n_pcol, col_blocks, slot...]
    reduce_max x3 -> x0, other arithmetic: 15.3 us -> none  [the longest x2 10.2 us: on_device(): col_part = jnp.max(scaled, axis=1) * alive[:, None]]
    another operation x6 -> x0, other arithmetic: 9.63 us -> none  [fold_rows(): return carry.at[places].max(pieces[1].reshape(-1, width))]
    gather x6 -> x0, local copies, waits for them, and re-layouts: 3.61 us -> none  [the longest x3 1.81 us: on_device(): row_vec[brow][:, :, None]]
    unnamed x2, local copies, waits for them, and re-layouts: 1.27 us -> 2.75 us
    convert_element_type x5 -> x0, other arithmetic: 1.36 us -> none  [the longest x1 0.66 us: on_device(): brow_float = brow.astype(jnp.float32).reshape(1, 1, slots)]
    select_n x4 -> x0, other arithmetic: 1.33 us -> none  [the longest x1 0.66 us: on_device(): row_vec[brow][:, :, None]]
where the time goes in v1:
time: 44.5 us; the launch traced here: 44.2 us
  Pallas kernels  40.2 us (90%)
  local copies, waits for them, and re-layouts  2.75 us (6%)
  between operations  1.29 us (3%)
    pallas_call x1, Pallas kernels, on_device(): pl.pallas_call(functools.partial(kernel, n_prow, n_pcol, col_blocks, slot...  40.2 us
    unnamed x2, local copies, waits for them, and re-layouts  2.75 us

profile of v1, /device:TPU:0, one launch (start us, length us, event | category | flops | bytes accessed | tf_op | source)
XLA Modules:
  0.0 44.2 jit_solution(14763496353722558010)
XLA Ops:
  1.3 40.2 %shard_map.59 = (f32[32,256]{1,0:T(8,128)}, f32[16,256]{1,0:T(8,128)}) custom-call(s32[32]{0:T(128)} %bitcast.10, s32[32]{0:T(128)} %bitcast.11, s32[1]{0:T(128)} %bitcast.6.count_ref, bf16[32,256,256]{2,1,0:T(8,128)(2,1)} %bitcast.7), custom_call_target="tpu_custom_call" | custom-call | tf_op jit(solution)/shard_map/pallas_call | solution.py:158
  41.5 1.4 %copy.6 = f32[32,1,256]{2,1,0:T(1,128)} copy(f32[32,1,256]{2,0,1:T(8,128)} %bitcast.8) | data formatting | bytes 65536
  42.9 1.3 %copy.7 = f32[16,1,256]{2,1,0:T(1,128)} copy(f32[16,1,256]{2,0,1:T(8,128)} %bitcast.9) | data formatting | bytes 32768

commit v2 on v1

v2 whole, which is shorter than its diff:
```python
import functools

import jax
import jax.numpy as jnp
from jax import lax
from jax.experimental import pallas as pl
from jax.experimental.pallas import tpu as pltpu
from jax.sharding import PartitionSpec as P

BR_DEV = 32
SWEEPS = 3
LANES = 128
STEP = 4
ROWS = 16


def rescale(scale, largest):
    return scale / jnp.sqrt(largest)


def kernel(
    n_prow, n_pcol, col_blocks, slots, width,
    brow_ref, bcol_ref, count_ref, tiles_ref,
    row_out, col_out,
    block, row_split, col_vec, spread_a, spread_b, peak_a, peak_b,
    row_send, pair_recv, half_send, half_recv, done_send, done_recv, col_send, col_recv,
    load_sem, pair_send_sem, pair_recv_sem, half_send_sem, half_recv_sem,
    done_send_sem, done_recv_sem, col_send_sem, col_recv_sem,
):
    def load(t):
        at = pl.ds(t * STEP, STEP)
        return pltpu.make_async_copy(tiles_ref.at[at], block.at[at], load_sem.at[t])

    for t in range(slots // STEP):
        load(t).start()

    pr = lax.axis_index("prow")
    pc = lax.axis_index("pcol")
    side = lax.rem(pc, 2)
    partner = pc + 1 - 2 * side
    barrier = pltpu.get_barrier_semaphore()
    pl.semaphore_signal(barrier, inc=1, device_id={"pcol": partner})
    for d in range(1, n_pcol // 2):
        pl.semaphore_signal(barrier, inc=1, device_id={"pcol": lax.rem(pc + 2 * d, n_pcol)})
    for d in range(1, n_prow):
        pl.semaphore_signal(barrier, inc=1, device_id={"prow": lax.rem(pr + d, n_prow)})

    count = count_ref[0]
    row_ids = lax.broadcasted_iota(jnp.int32, (BR_DEV, width), 0)
    col_ids = lax.broadcasted_iota(jnp.int32, (col_blocks, width), 0)
    lane_ids = lax.broadcasted_iota(jnp.int32, (1, LANES), 1)
    ones = jnp.ones((LANES, LANES), jnp.bfloat16)
    lane_full = lax.broadcasted_iota(jnp.int32, (8, LANES), 1)
    lane_group = lane_full // 8
    own_lane = lane_full % 8 == lax.broadcasted_iota(jnp.int32, (8, LANES), 0)
    halves = width // LANES
    peak_b[...] = jnp.zeros_like(peak_b)

    def spread_rows(s, out, j):
        brow = brow_ref[jnp.minimum(s, slots - 1)]
        pick = jnp.where(
            (lane_ids % BR_DEV == brow) & (lane_ids < 3 * BR_DEV), 1.0, 0.0
        ).astype(jnp.bfloat16)
        out[j] = jnp.dot(row_split[...] * pick, ones, preferred_element_type=jnp.float32)

    def scale_tile(s, spread, peak, j, col_acc):
        bcol = bcol_ref[s]
        if spread is not None:
            cols = col_vec[pl.ds(bcol, 1), :]
        col_part = [None] * halves
        for g in range(width // ROWS):
            at = slice(g * ROWS, (g + 1) * ROWS)
            best = None
            for h in range(halves):
                lanes = slice(h * LANES, (h + 1) * LANES)
                x = jnp.abs(block[s, at, lanes]).astype(jnp.float32)
                if spread is not None:
                    x = (x * spread[j, at, :]) * cols[:, lanes]
                col_part[h] = x if g == 0 else jnp.maximum(col_part[h], x)
                best = x if h == 0 else jnp.maximum(best, x)
            peak[j, at, :] = best
        top = jnp.concatenate([jnp.max(c, axis=0, keepdims=True) for c in col_part], axis=1)
        col_at = jnp.where(s < count, bcol, -1)
        return jnp.maximum(col_acc, jnp.where(col_ids == col_at, top, 0.0))

    def reduce_rows(s, peak, j, row_acc):
        parts = []
        for h in range(halves):
            packed = None
            for g in range(LANES // 8):
                at = h * LANES + 8 * g
                best = jnp.max(peak[j, at:at + 8, :], axis=1, keepdims=True)
                best = jnp.broadcast_to(best, (8, LANES))
                packed = best if g == 0 else jnp.where(lane_group == g, best, packed)
            parts.append(jnp.max(jnp.where(own_lane, packed, 0.0), axis=0, keepdims=True))
        row_at = jnp.where((s >= 0) & (s < count), brow_ref[jnp.maximum(s, 0)], -1)
        return jnp.maximum(
            row_acc, jnp.where(row_ids == row_at, jnp.concatenate(parts, axis=1), 0.0)
        )

    def four_tiles(t, carry, first):
        row_acc, col_acc = carry
        base = t * STEP
        if first:
            load(t).wait()
        for part in range(2):
            here, peak = (spread_a, peak_a) if part == 0 else (spread_b, peak_b)
            there, last = (spread_b, peak_b) if part == 0 else (spread_a, peak_a)
            s = base + 2 * part
            if not first:
                for j in range(2):
                    spread_rows(s + 2 + j, there, j)
            for j in range(2):
                row_acc = reduce_rows(s - 2 + j, last, j, row_acc)
            for j in range(2):
                col_acc = scale_tile(s + j, None if first else here, peak, j, col_acc)
        return row_acc, col_acc

    row_vec = jnp.ones((BR_DEV, width), jnp.float32)
    col_now = jnp.ones((col_blocks, width), jnp.float32)
    half = BR_DEV // 2
    for sweep in range(SWEEPS):
        if sweep > 0:
            for j in range(2):
                spread_rows(j, spread_a, j)
        row_max, col_max = lax.fori_loop(
            0, slots // STEP, functools.partial(four_tiles, first=sweep == 0),
            (jnp.zeros((BR_DEV, width), jnp.float32), jnp.zeros((col_blocks, width), jnp.float32)),
        )
        col_send[sweep] = col_max
        for j in range(2):
            row_max = reduce_rows(slots - 2 + j, peak_b, j, row_max)
        row_send[sweep, 0] = row_max[:half]
        row_send[sweep, 1] = row_max[half:]
        if sweep == 0:
            pl.semaphore_wait(barrier, n_pcol // 2 + n_prow - 1)
        pair = pltpu.make_async_remote_copy(
            src_ref=row_send.at[sweep, 1 - side], dst_ref=pair_recv.at[sweep],
            send_sem=pair_send_sem.at[sweep], recv_sem=pair_recv_sem.at[sweep],
            device_id={"pcol": partner},
        )
        pair.start()
        col_copies = []
        for d in range(1, n_prow):
            col_copies.append(pltpu.make_async_remote_copy(
                src_ref=col_send.at[sweep], dst_ref=col_recv.at[sweep, d - 1],
                send_sem=col_send_sem.at[sweep, d - 1], recv_sem=col_recv_sem.at[sweep, d - 1],
                device_id={"prow": lax.rem(pr + d, n_prow)},
            ))
        for copy in col_copies:
            copy.start()
        mine = row_send[sweep, side]
        pair.wait()
        mine = jnp.maximum(mine, pair_recv[sweep])
        half_send[sweep] = mine
        half_copies = []
        for d in range(1, n_pcol // 2):
            half_copies.append(pltpu.make_async_remote_copy(
                src_ref=half_send.at[sweep], dst_ref=half_recv.at[sweep, d - 1],
                send_sem=half_send_sem.at[sweep, d - 1], recv_sem=half_recv_sem.at[sweep, d - 1],
                device_id={"pcol": lax.rem(pc + 2 * d, n_pcol)},
            ))
        for copy in half_copies:
            copy.start()
        for d, copy in enumerate(half_copies):
            copy.wait()
            mine = jnp.maximum(mine, half_recv[sweep, d])
        done_send[sweep] = mine
        done = pltpu.make_async_remote_copy(
            src_ref=done_send.at[sweep], dst_ref=done_recv.at[sweep],
            send_sem=done_send_sem.at[sweep], recv_sem=done_recv_sem.at[sweep],
            device_id={"pcol": partner},
        )
        done.start()
        for d, copy in enumerate(col_copies):
            copy.wait()
            col_max = jnp.maximum(col_max, col_recv[sweep, d])
        col_now = rescale(col_now, col_max)
        done.wait()
        other = done_recv[sweep]
        row_max = jnp.concatenate(
            [jnp.where(side == 0, mine, other), jnp.where(side == 0, other, mine)], axis=0
        )
        row_vec = rescale(row_vec, row_max)
        if sweep + 1 < SWEEPS:
            col_vec[...] = col_now
            top = row_vec.astype(jnp.bfloat16).astype(jnp.float32)
            left = row_vec - top
            mid = left.astype(jnp.bfloat16).astype(jnp.float32)
            low = left - mid
            rest = jnp.zeros((LANES - 3 * BR_DEV, width), jnp.float32)
            stack = jnp.concatenate([top, mid, low, rest], axis=0)
            for h in range(halves):
                row_split[h * LANES:(h + 1) * LANES, :] = (
                    stack[:, h * LANES:(h + 1) * LANES].T.astype(jnp.bfloat16)
                )
    row_out[...] = row_vec
    col_out[...] = col_now


def spell(row_ref, col_ref, row_out, col_out):
    for ref, out in ((row_ref, row_out), (col_ref, col_out)):
        for i in range(ref.shape[0]):
            out[i] = ref[i:i + 1, :]


def solution(mesh):
    n_prow, n_pcol = mesh.shape["prow"], mesh.shape["pcol"]

    def on_device(tiles, tile_brow, tile_bcol, tile_count):
        slots, width = tiles.shape[2], tiles.shape[3]
        col_blocks = BR_DEV * n_prow // n_pcol
        half = BR_DEV // 2
        smem = pl.BlockSpec(memory_space=pltpu.SMEM)
        vmem = pl.BlockSpec(memory_space=pltpu.VMEM)
        row_vec, col_vec = pl.pallas_call(
            functools.partial(kernel, n_prow, n_pcol, col_blocks, slots, width),
            out_shape=(
                jax.ShapeDtypeStruct((BR_DEV, width), jnp.float32),
                jax.ShapeDtypeStruct((col_blocks, width), jnp.float32),
            ),
            in_specs=[smem, smem, smem, pl.BlockSpec(memory_space=pl.ANY)],
            out_specs=(vmem, vmem),
            scratch_shapes=[
                pltpu.VMEM((slots, width, width), jnp.bfloat16),
                pltpu.VMEM((width, LANES), jnp.bfloat16),
                pltpu.VMEM((col_blocks, width), jnp.float32),
                pltpu.VMEM((2, width, LANES), jnp.float32),
                pltpu.VMEM((2, width, LANES), jnp.float32),
                pltpu.VMEM((2, width, LANES), jnp.float32),
                pltpu.VMEM((2, width, LANES), jnp.float32),
                pltpu.VMEM((SWEEPS, 2, half, width), jnp.float32),
                pltpu.VMEM((SWEEPS, half, width), jnp.float32),
                pltpu.VMEM((SWEEPS, half, width), jnp.float32),
                pltpu.VMEM((SWEEPS, n_pcol // 2 - 1, half, width), jnp.float32),
                pltpu.VMEM((SWEEPS, half, width), jnp.float32),
                pltpu.VMEM((SWEEPS, half, width), jnp.float32),
                pltpu.VMEM((SWEEPS, col_blocks, width), jnp.float32),
                pltpu.VMEM((SWEEPS, n_prow - 1, col_blocks, width), jnp.float32),
                pltpu.SemaphoreType.DMA((slots // STEP,)),
                pltpu.SemaphoreType.DMA((SWEEPS,)),
                pltpu.SemaphoreType.DMA((SWEEPS,)),
                pltpu.SemaphoreType.DMA((SWEEPS, n_pcol // 2 - 1)),
                pltpu.SemaphoreType.DMA((SWEEPS, n_pcol // 2 - 1)),
                pltpu.SemaphoreType.DMA((SWEEPS,)),
                pltpu.SemaphoreType.DMA((SWEEPS,)),
                pltpu.SemaphoreType.DMA((SWEEPS, n_prow - 1)),
                pltpu.SemaphoreType.DMA((SWEEPS, n_prow - 1)),
            ],
            compiler_params=pltpu.CompilerParams(collective_id=0, has_side_effects=True),
        )(
            tile_brow.reshape(slots), tile_bcol.reshape(slots), tile_count.reshape(1),
            tiles.reshape(slots, width, width),
        )
        return pl.pallas_call(
            spell,
            out_shape=(
                jax.ShapeDtypeStruct((BR_DEV, 1, width), jnp.float32),
                jax.ShapeDtypeStruct((col_blocks, 1, width), jnp.float32),
            ),
            in_specs=[vmem, vmem],
            out_specs=(vmem, vmem),
        )(row_vec, col_vec)

    return jax.shard_map(
        on_device,
        mesh=mesh,
        in_specs=(
            P("prow", "pcol", None, None, None),
            P("prow", "pcol", None),
            P("prow", "pcol", None),
            P("prow", "pcol"),
        ),
        out_specs=(P(None, "prow", None), P(None, "pcol", None)),
        check_vma=False,
    )
```

time: 44.5 us -> 31.9 us (0.72)
  Pallas kernels: 40.2 us -> 30.4 us
  local copies, waits for them, and re-layouts: 2.75 us -> 0 us
    pallas_call x1, Pallas kernels: 40.2 us -> 29 us  [on_device(): pl.pallas_call(functools.partial(kernel, n_prow, n_pcol, col_blocks, slot...]
    unnamed x2 -> x0, local copies, waits for them, and re-layouts: 2.75 us -> none
    pallas_call x0 -> x1, Pallas kernels: none -> 1.4 us  [on_device(): pl.pallas_call(spell, out_shape=(jax.ShapeDtypeStruct((BR_DEV, 1, width),...]
where the time goes in v2:
time: 31.9 us; the launch traced here: 31.7 us
  Pallas kernels  30.4 us (95%)
  between operations  1.29 us (4%)
    pallas_call x1, Pallas kernels, on_device(): pl.pallas_call(functools.partial(kernel, n_prow, n_pcol, col_blocks, slot...  29 us
    pallas_call x1, Pallas kernels, on_device(): pl.pallas_call(spell, out_shape=(jax.ShapeDtypeStruct((BR_DEV, 1, width),...  1.4 us

profile of v2, /device:TPU:0, one launch (start us, length us, event | category | flops | bytes accessed | tf_op | source)
XLA Modules:
  0.0 31.7 jit_solution(13149042232517242352)
XLA Ops:
  1.3 29.0 %shard_map.59 = (f32[32,256]{1,0:T(8,128)}, f32[16,256]{1,0:T(8,128)}) custom-call(s32[32]{0:T(128)} %bitcast.6, s32[32]{0:T(128)} %bitcast.7, s32[1]{0:T(128)} %bitcast.4.count_ref, bf16[32,256,256]{2,1,0:T(8,128)(2,1)} %bitcast.5), custom_call_target="tpu_custom_call" | custom-call | tf_op jit(solution)/shard_map/pallas_call | solution.py:216
  30.3 1.4 %shard_map.60 = (f32[32,1,256]{2,1,0:T(1,128)}, f32[16,1,256]{2,1,0:T(1,128)}) custom-call(f32[32,256]{1,0:T(8,128)} %get-tuple-element.4.row_ref, f32[16,256]{1,0:T(8,128)} %get-tuple-element.5.col_ref), custom_call_target="tpu_custom_call" | custom-call | tf_op jit(solution)/shard_map/pallas_call | solution.py:255

commit v3 on v2

--- a/solution.py
+++ b/solution.py
@@ -23,8 +23,8 @@
     brow_ref, bcol_ref, count_ref, tiles_ref,
     row_out, col_out,
     block, row_split, col_vec, spread_a, spread_b, peak_a, peak_b,
-    row_send, pair_recv, half_send, half_recv, done_send, done_recv, col_send, col_recv,
-    load_sem, pair_send_sem, pair_recv_sem, half_send_sem, half_recv_sem,
+    row_send, part_recv, done_send, done_recv, col_send, col_recv,
+    load_sem, part_send_sem, part_recv_sem,
     done_send_sem, done_recv_sem, col_send_sem, col_recv_sem,
 ):
     def load(t):
@@ -36,12 +36,9 @@
 
     pr = lax.axis_index("prow")
     pc = lax.axis_index("pcol")
-    side = lax.rem(pc, 2)
-    partner = pc + 1 - 2 * side
     barrier = pltpu.get_barrier_semaphore()
-    pl.semaphore_signal(barrier, inc=1, device_id={"pcol": partner})
-    for d in range(1, n_pcol // 2):
-        pl.semaphore_signal(barrier, inc=1, device_id={"pcol": lax.rem(pc + 2 * d, n_pcol)})
+    for d in range(1, n_pcol):
+        pl.semaphore_signal(barrier, inc=1, device_id={"pcol": lax.rem(pc + d, n_pcol)})
     for d in range(1, n_prow):
         pl.semaphore_signal(barrier, inc=1, device_id={"prow": lax.rem(pr + d, n_prow)})
 
@@ -118,7 +115,7 @@
 
     row_vec = jnp.ones((BR_DEV, width), jnp.float32)
     col_now = jnp.ones((col_blocks, width), jnp.float32)
-    half = BR_DEV // 2
+    share = BR_DEV // n_pcol
     for sweep in range(SWEEPS):
         if sweep > 0:
             for j in range(2):
@@ -130,16 +127,19 @@
         col_send[sweep] = col_max
         for j in range(2):
             row_max = reduce_rows(slots - 2 + j, peak_b, j, row_max)
-        row_send[sweep, 0] = row_max[:half]
-        row_send[sweep, 1] = row_max[half:]
+        row_send[sweep] = row_max
         if sweep == 0:
-            pl.semaphore_wait(barrier, n_pcol // 2 + n_prow - 1)
-        pair = pltpu.make_async_remote_copy(
-            src_ref=row_send.at[sweep, 1 - side], dst_ref=pair_recv.at[sweep],
-            send_sem=pair_send_sem.at[sweep], recv_sem=pair_recv_sem.at[sweep],
-            device_id={"pcol": partner},
-        )
-        pair.start()
+            pl.semaphore_wait(barrier, n_pcol - 1 + n_prow - 1)
+        part_copies = []
+        for d in range(1, n_pcol):
+            to = lax.rem(pc + d, n_pcol)
+            part_copies.append(pltpu.make_async_remote_copy(
+                src_ref=row_send.at[sweep], dst_ref=part_recv.at[sweep, d - 1],
+                send_sem=part_send_sem.at[sweep, d - 1], recv_sem=part_recv_sem.at[sweep, d - 1],
+                device_id={"pcol": to},
+            ))
+        for copy in part_copies:
+            copy.start()
         col_copies = []
         for d in range(1, n_prow):
             col_copies.append(pltpu.make_async_remote_copy(
@@ -149,38 +149,13 @@
             ))
         for copy in col_copies:
             copy.start()
-        mine = row_send[sweep, side]
-        pair.wait()
-        mine = jnp.maximum(mine, pair_recv[sweep])
-        half_send[sweep] = mine
-        half_copies = []
-        for d in range(1, n_pcol // 2):
-            half_copies.append(pltpu.make_async_remote_copy(
-                src_ref=half_send.at[sweep], dst_ref=half_recv.at[sweep, d - 1],
-                send_sem=half_send_sem.at[sweep, d - 1], recv_sem=half_recv_sem.at[sweep, d - 1],
-                device_id={"pcol": lax.rem(pc + 2 * d, n_pcol)},
-            ))
-        for copy in half_copies:
-            copy.start()
-        for d, copy in enumerate(half_copies):
-            copy.wait()
-            mine = jnp.maximum(mine, half_recv[sweep, d])
-        done_send[sweep] = mine
-        done = pltpu.make_async_remote_copy(
-            src_ref=done_send.at[sweep], dst_ref=done_recv.at[sweep],
-            send_sem=done_send_sem.at[sweep], recv_sem=done_recv_sem.at[sweep],
-            device_id={"pcol": partner},
-        )
-        done.start()
         for d, copy in enumerate(col_copies):
             copy.wait()
             col_max = jnp.maximum(col_max, col_recv[sweep, d])
         col_now = rescale(col_now, col_max)
-        done.wait()
-        other = done_recv[sweep]
-        row_max = jnp.concatenate(
-            [jnp.where(side == 0, mine, other), jnp.where(side == 0, other, mine)], axis=0
-        )
+        for d, copy in enumerate(part_copies):
+            copy.wait()
+            row_max = jnp.maximum(row_max, part_recv[sweep, d])
         row_vec = rescale(row_vec, row_max)
         if sweep + 1 < SWEEPS:
             col_vec[...] = col_now
@@ -210,7 +185,7 @@
     def on_device(tiles, tile_brow, tile_bcol, tile_count):
         slots, width = tiles.shape[2], tiles.shape[3]
         col_blocks = BR_DEV * n_prow // n_pcol
-        half = BR_DEV // 2
+        share = BR_DEV // n_pcol
         smem = pl.BlockSpec(memory_space=pltpu.SMEM)
         vmem = pl.BlockSpec(memory_space=pltpu.VMEM)
         row_vec, col_vec = pl.pallas_call(
@@ -229,21 +204,17 @@
                 pltpu.VMEM((2, width, LANES), jnp.float32),
                 pltpu.VMEM((2, width, LANES), jnp.float32),
                 pltpu.VMEM((2, width, LANES), jnp.float32),
-                pltpu.VMEM((SWEEPS, 2, half, width), jnp.float32),
-                pltpu.VMEM((SWEEPS, half, width), jnp.float32),
-                pltpu.VMEM((SWEEPS, half, width), jnp.float32),
-                pltpu.VMEM((SWEEPS, n_pcol // 2 - 1, half, width), jnp.float32),
-                pltpu.VMEM((SWEEPS, half, width), jnp.float32),
-                pltpu.VMEM((SWEEPS, half, width), jnp.float32),
+                pltpu.VMEM((SWEEPS, BR_DEV, width), jnp.float32),
+                pltpu.VMEM((SWEEPS, n_pcol - 1, BR_DEV, width), jnp.float32),
+                pltpu.VMEM((SWEEPS, share, width), jnp.float32),
+                pltpu.VMEM((SWEEPS, n_pcol, share, width), jnp.float32),
                 pltpu.VMEM((SWEEPS, col_blocks, width), jnp.float32),
                 pltpu.VMEM((SWEEPS, n_prow - 1, col_blocks, width), jnp.float32),
                 pltpu.SemaphoreType.DMA((slots // STEP,)),
-                pltpu.SemaphoreType.DMA((SWEEPS,)),
-                pltpu.SemaphoreType.DMA((SWEEPS,)),
-                pltpu.SemaphoreType.DMA((SWEEPS, n_pcol // 2 - 1)),
-                pltpu.SemaphoreType.DMA((SWEEPS, n_pcol // 2 - 1)),
-                pltpu.SemaphoreType.DMA((SWEEPS,)),
-                pltpu.SemaphoreType.DMA((SWEEPS,)),
+                pltpu.SemaphoreType.DMA((SWEEPS, n_pcol - 1)),
+                pltpu.SemaphoreType.DMA((SWEEPS, n_pcol - 1)),
+                pltpu.SemaphoreType.DMA((SWEEPS, n_pcol - 1)),
+                pltpu.SemaphoreType.DMA((SWEEPS, n_pcol - 1)),
                 pltpu.SemaphoreType.DMA((SWEEPS, n_prow - 1)),
                 pltpu.SemaphoreType.DMA((SWEEPS, n_prow - 1)),
             ],

time: 31.9 us -> 31.1 us (0.975)
  Pallas kernels: 30.4 us -> 29.6 us
    pallas_call x1, Pallas kernels: 29 us -> 28.2 us  [on_device(): pl.pallas_call(functools.partial(kernel, n_prow, n_pcol, col_blocks, slot...]
where the time goes in v3:
time: 31.1 us; the launch traced here: 30.9 us
  Pallas kernels  29.6 us (95%)
  between operations  1.29 us (4%)
    pallas_call x1, Pallas kernels, on_device(): pl.pallas_call(functools.partial(kernel, n_prow, n_pcol, col_blocks, slot...  28.2 us
    pallas_call x1, Pallas kernels, on_device(): pl.pallas_call(spell, out_shape=(jax.ShapeDtypeStruct((BR_DEV, 1, width),...  1.4 us

profile of v3, /device:TPU:0, one launch (start us, length us, event | category | flops | bytes accessed | tf_op | source)
XLA Modules:
  0.0 30.9 jit_solution(15145041170249086329)
XLA Ops:
  1.3 28.2 %shard_map.59 = (f32[32,256]{1,0:T(8,128)}, f32[16,256]{1,0:T(8,128)}) custom-call(s32[32]{0:T(128)} %bitcast.6, s32[32]{0:T(128)} %bitcast.7, s32[1]{0:T(128)} %bitcast.4.count_ref, bf16[32,256,256]{2,1,0:T(8,128)(2,1)} %bitcast.5), custom_call_target="tpu_custom_call" | custom-call | tf_op jit(solution)/shard_map/pallas_call | solution.py:191
  29.5 1.4 %shard_map.60 = (f32[32,1,256]{2,1,0:T(1,128)}, f32[16,1,256]{2,1,0:T(1,128)}) custom-call(f32[32,256]{1,0:T(8,128)} %get-tuple-element.4.row_ref, f32[16,256]{1,0:T(8,128)} %get-tuple-element.5.col_ref), custom_call_target="tpu_custom_call" | custom-call | tf_op jit(solution)/shard_map/pallas_call | solution.py:226
